TPU v7x, 32 devices: a whole 2x2x4 slice. The times are simulated.
32 devices in a mesh: node: 8 (over y, x, core), chip: 4 (over z).
Axes of the slice: x: 2, y: 2, z: 4, core: 2. Of those that a mesh axis runs over, the one named last changes fastest.
Arguments:
- momentum: float32 [32, 128, 512], P(('node', 'chip')), may hold values from -6 to 6
- gradient: bfloat16 [32, 128, 512], P(('node', 'chip')), may hold values from -6 to 6
- indices: int32 [32, 16, 32], P(('node', 'chip')), may hold values from 0 to 4095, as said below
Outputs:
- new_momentum: float32 [32, 128, 512], P(('node', 'chip'))
- update: float32 [128, 512], replicated
Inputs may be any that keep to these rules, and one draw needn't show every extreme that they name: `indices`: the 32 entries of each row name distinct coefficients of their span, coefficient (k, l) being k * 64 + l.
All inputs are finite; a program needn't handle non-finite values.
Results may differ from a plain program's by a relative error of at most 0.0029.
Values may be sent and summed in bfloat16 or wider, within the bound.
A program may use at most 64 MiB of HBM per device.

v0:
```python
import math

import jax
import jax.numpy as jnp
from jax import lax
from jax.sharding import PartitionSpec as P

SPAN = 64


def dct_table(edge_len):
    orders = jnp.arange(edge_len, dtype=jnp.float32)
    wave_no = orders[:, None]
    cell_no = orders[None, :]
    factor = jnp.where(wave_no == 0.0, math.sqrt(1.0 / edge_len), math.sqrt(2.0 / edge_len))
    return factor * jnp.cos(math.pi * (2.0 * cell_no + 1.0) * wave_no / (2.0 * edge_len))


def forward(grid_field, cosines, edge_len):
    row_blocks = grid_field.shape[0] // edge_len
    col_blocks = grid_field.shape[1] // edge_len
    blocks = grid_field.reshape(row_blocks, edge_len, col_blocks, edge_len).transpose(0, 2, 1, 3)
    coeffs = jnp.einsum(
        "kn,abnm,lm->abkl", cosines, blocks, cosines, precision=lax.Precision.HIGHEST
    )
    return coeffs.reshape(row_blocks * col_blocks, edge_len * edge_len)


def inverse_blocks(coeffs, cosines, edge_len):
    blocks = coeffs.reshape(coeffs.shape[0], edge_len, edge_len)
    return jnp.einsum("kn,ckl,lm->cnm", cosines, blocks, cosines, precision=lax.Precision.HIGHEST)


def place_blocks(blocks, row_count, col_count, edge_len):
    shaped = blocks.reshape(row_count // edge_len, col_count // edge_len, edge_len, edge_len)
    return shaped.transpose(0, 2, 1, 3).reshape(row_count, col_count)


def normalized(blocks):
    energy = jnp.mean(blocks * blocks, axis=(1, 2), keepdims=True)
    return blocks / jnp.sqrt(energy + 1.0)


def decode_block(picked, slots):
    n_spans = picked.shape[1]
    values_rows = jnp.moveaxis(picked, 1, 0).reshape(n_spans, -1)
    slot_rows = jnp.moveaxis(slots, 1, 0).reshape(n_spans, -1)
    orders = jnp.arange(SPAN, dtype=jnp.int32)[None, :]

    def one_span(pair):
        vals, where = pair
        wave_rows = (where // SPAN)[:, None] == orders
        wave_cols = (where % SPAN)[:, None] == orders
        left_hot = wave_rows.astype(jnp.bfloat16)
        right_hot = jnp.where(wave_cols, vals[:, None], jnp.zeros((), jnp.bfloat16))
        block = lax.dot_general(
            left_hot, right_hot, (((0,), (0,)), ((), ())), preferred_element_type=jnp.float32
        )
        return block.reshape(SPAN * SPAN)

    return lax.map(one_span, (values_rows, slot_rows))


def decode_lists(totals, picked, slots):
    count = picked.shape[0]
    group_len = 1
    for trial in range(1, 17):
        if count % trial == 0:
            group_len = trial
    picked_groups = picked.reshape((count // group_len, group_len) + picked.shape[1:])
    slot_groups = slots.reshape((count // group_len, group_len) + slots.shape[1:])

    def add_group(step, carry):
        return carry + decode_block(picked_groups[step], slot_groups[step])

    return lax.fori_loop(0, count // group_len, add_group, totals)


def shards(momentum, gradient, indices):
    cosines = dct_table(SPAN)
    row_count = momentum.shape[1]
    col_count = momentum.shape[2]
    blended = 0.9 * momentum[0] + gradient[0].astype(jnp.float32)
    coeffs = forward(blended, cosines, SPAN)
    slots = indices[0]
    picked = jnp.take_along_axis(coeffs, slots, axis=1).astype(jnp.bfloat16)
    sparse = decode_block(picked[None], indices)
    own_part = place_blocks(inverse_blocks(sparse, cosines, SPAN), row_count, col_count, SPAN)
    new_momentum = (blended - own_part)[None]
    partial_sum = decode_lists(
        jnp.zeros_like(coeffs),
        lax.all_gather(picked[None], "chip", axis=0, tiled=True),
        lax.all_gather(indices, "chip", axis=0, tiled=True),
    )
    totals = lax.psum(partial_sum, "node")
    update = place_blocks(
        normalized(inverse_blocks(totals, cosines, SPAN)), row_count, col_count, SPAN
    )
    return (new_momentum, update)


def solution(mesh):
    return jax.shard_map(
        shards,
        mesh=mesh,
        in_specs=(
            P(("node", "chip"), None, None),
            P(("node", "chip"), None, None),
            P(("node", "chip"), None, None),
        ),
        out_specs=(P(("node", "chip"), None, None), P()),
        check_vma=False,
    )
```

profile of v0, /device:TPU:0, one launch (start us, length us, event | category | flops | bytes accessed | tf_op | source)
XLA Modules:
  0.0 127.8 jit_solution(4356147614158876346)
XLA Ops:
  7.2 0.8 fusion.53
  8.0 14.8 %all_gather.6 = s32[4,16,32]{2,1,0:T(8,128)S(1)} all-gather(s32[1,16,32]{2,1,0:T(8,128)S(1)} %copy-done), channel_id=1, replica_groups=mesh['node'=8,'chip'=4] {'chip'}, dimensions={0}, use_global_device_ids=true | all-gather | bytes 10240 | tf_op jit(solution)/shard_map/all_gather | solution.py:93
  22.8 1.1 convert_add_fusion
  24.3 1.7 %fusion.20 = f32[2,8,64,64]{2,3,1,0:T(8,128)S(1)} fusion(f32[2,64,8,64]{1,3,2,0:T(8,128)S(1)} %copy.20, f32[64]{0:T(128)S(1)} %get-tuple-element.232, f32[64]{0:T(128)S(1)} %get-tuple-element.231), kind=kOutput, calls=%fused_computation.37 | convolution fusion | flops 50343936 | bytes 524800 | tf_op jit(solution)/shard_map/kn,abnm,lm->abkl/dot_general | solution.py:23
  26.0 0.7 fusion.22
  27.0 4.8 %gather_fusion = bf16[512]{0:T(512)(128)(2,1)S(1)} fusion(bf16[16,4096]{1,0:T(8,128)(2,1)S(1)} %reshape.216, s32[512]{0:T(512)S(1)} %reshape.225), kind=kCustom, calls=%fused_computation | custom fusion | bytes 6144 | tf_op jit(solution)/shard_map/jit(take_along_axis)/gather | solution.py:86
  32.0 13.2 %all_gather.7 = bf16[4,16,32]{2,1,0:T(8,128)(2,1)S(1)} all-gather(bf16[1,16,32]{2,1,0:T(8,128)(2,1)S(1)} %select_convert_fusion), channel_id=1, replica_groups=mesh['node'=8,'chip'=4] {'chip'}, dimensions={0}, use_global_device_ids=true | all-gather | bytes 5120 | tf_op jit(solution)/shard_map/all_gather | solution.py:92
  45.4 13.3 %while.37 = (s32[]{:T(128)}, f32[16,4096]{1,0:T(8,128)S(1)}, s32[16,128]{1,0:T(8,128)S(1)}, bf16[16,128]{1,0:T(8,128)(2,1)S(1)}, s32[]{:T(128)}, /*index=5*/s32[]{:T(128)}) while((s32[]{:T(128)}, f32[16,4096]{1,0:T(8,128)S(1)}, s32[16,128]{1,0:T(8,128)S(1)}, bf16[16,128]{1,0:T(8,128)(2,1)S(1)}, s32[]{:T(128)}, ...), condition=%wide.region_3.4_spmd.clone.clone, body=%wide.region_2.3_spmd.clone.clone.sunk | while | flops 1075714 | bytes 86353 | solution.py:61
  45.8 0.4 dynamic_update_slice.20
  47.5 0.4 dynamic_update_slice.20
  48.3 0.4 dynamic_update_slice.20
  50.8 0.4 dynamic_update_slice.20
  51.7 0.4 dynamic_update_slice.20
  54.1 0.4 dynamic_update_slice.20
  55.0 0.4 dynamic_update_slice.20
  57.5 0.4 dynamic_update_slice.20
  58.3 0.4 dynamic_update_slice.20
  58.9 1.0 copy.27
  60.1 13.3 %while.36 = (s32[]{:T(128)}, f32[16,4096]{1,0:T(8,128)S(1)}, s32[16,32]{1,0:T(8,128)S(1)}, bf16[16,32]{1,0:T(8,128)(2,1)S(1)}, s32[]{:T(128)}, /*index=5*/s32[]{:T(128)}) while((s32[]{:T(128)}, f32[16,4096]{1,0:T(8,128)S(1)}, s32[16,32]{1,0:T(8,128)S(1)}, bf16[16,32]{1,0:T(8,128)(2,1)S(1)}, s32[]{:T(128)}, ...), condition=%wide.region_1.2_spmd.clone.clone, body=%wide.region_0.1_spmd.clone.clone.sunk | while | flops 268930 | bytes 83089 | solution.py:61
  61.3 0.4 dynamic_update_slice.19
  62.2 0.4 dynamic_update_slice.19
  63.8 0.4 dynamic_update_slice.19
  64.7 0.4 dynamic_update_slice.19
  65.5 0.4 dynamic_update_slice.19
  67.2 0.4 dynamic_update_slice.19
  73.6 0.7 fusion.31
  74.4 0.7 fusion.29
  75.5 0.7 sub.16
  76.3 39.7 %all-reduce.2.cloned.1.call-done = f32[16,64,64]{1,2,0:T(8,128)} async-done(((f32[16,64,64]{1,2,0:T(8,128)}), f32[16,64,64]{1,2,0:T(8,128)}) %all-reduce.2.cloned.1.call-update) | async-done | bytes 262160 | tf_op jit(solution)/shard_map/psum | solution.py:95
  116.0 2.8 %fusion.27 = f32[16,64,64]{1,2,0:T(8,128)S(1)} fusion(f32[16,64,64]{1,2,0:T(8,128)} %all-reduce.2.cloned.1.call-done, f32[64]{0:T(128)S(1)} %get-tuple-element.232, f32[64]{0:T(128)S(1)} %get-tuple-element.231), kind=kOutput, calls=%fused_computation.47 | convolution fusion | flops 50343936 | bytes 524800 | tf_op jit(solution)/shard_map/kn,ckl,lm->cnm/dot_general | solution.py:31
  118.8 0.8 multiply_reduce_fusion
  120.1 0.9 reshape.224
  (203 shorter events, 21.6 us)
Async XLA Ops:
  7.2 108.9 %all-reduce.2.cloned.1.call-start = ((), (), s32[]{:S(2)}) async-start(), calls=%async_computation | async-start | bytes 1048576 | tf_op jit(solution)/shard_map/psum | solution.py:95
  7.2 0.8 copy-start
Sparse Core Ops, SparseCore 0:
  60.1 55.8 all-reduce.1
where the time goes:
time: 128 us
  waiting for transfers between devices  39.8 us (31%)
  blocking collectives  28 us (22%)
  local copies, waits for them, and re-layouts  24.9 us (19%)
  matrix products  15.8 us (12%)
  between operations  14.2 us (11%)
  other arithmetic  3.41 us (3%)
  loops' own time  1.61 us (1%)
    psum x1, waiting for transfers between devices, shards(): totals = lax.psum(partial_sum, 'node')  39.7 us
    all_gather x1, blocking collectives, shards(): lax.all_gather(indices, 'chip', axis=0, tiled=True)  14.8 us
    all_gather x1, blocking collectives, shards(): lax.all_gather(picked[None], 'chip', axis=0, tiled=True)  13.2 us
    dynamic_update_slice x32, local copies, waits for them, and re-layouts, decode_block(): return lax.map(one_span, (values_rows, slot_rows))  12.6 us
    dot_general x32, matrix products, one_span(): lax.dot_general(left_hot, right_hot, (((0,), (0,)), ((), ())), preferred_...  8.39 us
    gather x4, local copies, waits for them, and re-layouts, shards(): picked = jnp.take_along_axis(coeffs, slots, axis=1).astype(jnp.bfloat16)  5.09 us
    dot_general x4, matrix products, inverse_blocks(): jnp.einsum('kn,ckl,lm->cnm', cosines, blocks, cosines, precision=lax.Prec...  5.02 us
    broadcast_in_dim x32, local copies, waits for them, and re-layouts, decode_block(): return lax.map(one_span, (values_rows, slot_rows))  2.91 us
  transfers between devices with their start and end apart: 1, of which 1 were waited for; matrix products, arithmetic and copies ran while one was open for 12% of the time, Pallas kernels for 0%

commit v1 on v0

v1 whole, which is shorter than its diff:
```python
import functools
import math

import jax
import jax.numpy as jnp
import numpy as np
from jax import lax
from jax.experimental import pallas as pl
from jax.experimental.pallas import tpu as pltpu
from jax.sharding import PartitionSpec as P

SPAN = 64
LANES = 128
MESH = pl.DeviceIdType.MESH
F32 = jnp.float32
BF16 = jnp.bfloat16


def cosine_blocks(copies):
    orders = np.arange(SPAN, dtype=np.float64)
    wave, cell = orders[:, None], orders[None, :]
    factor = np.where(wave == 0, math.sqrt(1 / SPAN), math.sqrt(2 / SPAN))
    table = factor * np.cos(math.pi * (2 * cell + 1) * wave / (2 * SPAN))
    full = np.kron(np.eye(copies), table)
    high = full.astype(BF16)
    low = (full - high.astype(np.float64)).astype(BF16)
    return np.stack([high.T, low.T, high, low])


def halves(x):
    high = x.astype(BF16)
    return high, (x - high.astype(F32)).astype(BF16)


def mm(a, b):
    return lax.dot_general(a, b, (((1,), (0,)), ((), ())), preferred_element_type=F32)


def mm_nt(a, b):
    return lax.dot_general(a, b, (((1,), (1,)), ((), ())), preferred_element_type=F32)


def both_sides(blocks, left, right, exact):
    outs = []
    for x in blocks:
        if exact:
            y = mm(x, right[0]) + mm(x, right[1])
        else:
            high, low = halves(x)
            y = mm(high, right[0]) + (mm(low, right[0]) + mm(high, right[1]))
        high, low = halves(y)
        outs.append(mm(left[0], high) + (mm(left[0], low) + mm(left[1], high)))
    return outs


def kernel(
    nodes, chips, topk, mom_hbm, grad_hbm, idx_hbm, cos_hbm, new_hbm, upd_hbm,
    mom, grad, idx, cos, new_out, upd, box, recv, acc, in_sem, out_sem, send_sem, recv_sem,
):
    node, chip = lax.axis_index("node"), lax.axis_index("chip")
    count = nodes * chips
    rows, cols = mom.shape
    per = LANES // topk
    wide = per * SPAN
    groups = idx.shape[0] // per
    strips = cols // wide
    used = 3 * groups

    loads = [
        pltpu.make_async_copy(src, dst, in_sem.at[i])
        for i, (src, dst) in enumerate(
            ((idx_hbm.at[0], idx), (mom_hbm.at[0], mom), (grad_hbm.at[0], grad), (cos_hbm, cos))
        )
    ]
    for load in loads:
        load.start()

    barrier = pltpu.get_barrier_semaphore()

    def peers(visit):
        def one(off, i):
            to_node = lax.rem(node + i, nodes)
            to_chip = lax.rem(chip + off, chips)
            visit(off, {"node": to_node, "chip": to_chip})

        order = sorted(range(chips), key=lambda o: -min(o, chips - o))
        for off in order:
            first = 1 if off == 0 else 0
            if nodes <= 8:
                for i in range(first, nodes):
                    one(off, i)
            else:
                pl.loop(first, nodes)(functools.partial(one, off))

    peers(lambda off, to: pl.semaphore_signal(barrier, inc=1, device_id=to, device_id_type=MESH))

    loads[0].wait()
    slots = idx[...]
    spans = slots.shape[0]
    lane = lax.broadcasted_iota(jnp.int32, (spans, LANES), 1)
    place = lax.broadcasted_iota(jnp.int32, (spans, LANES), 0) % per
    spread = jnp.concatenate([slots] * per, axis=1)
    spread = jnp.where(lane // topk == place, spread + place * (SPAN * SPAN), 0)
    lists = [
        jnp.sum(spread[g * per:(g + 1) * per], axis=0, keepdims=True) for g in range(groups)
    ]
    wave = [(x // SPAN) % SPAN for x in lists]
    wide_pos = [(x // (SPAN * SPAN)) * SPAN + x % SPAN for x in lists]
    tall_iota = lax.broadcasted_iota(jnp.int32, (SPAN, LANES), 0)
    wide_iota = lax.broadcasted_iota(jnp.int32, (wide, LANES), 0)
    wave_hot = [(tall_iota == w).astype(F32) for w in wave]
    wide_hot = [(wide_iota == w).astype(F32).astype(BF16) for w in wide_pos]

    for load in loads[1:]:
        load.wait()
    blended = 0.9 * mom[...] + grad[...].astype(F32)
    fwd_right = (cos[0], cos[1])
    fwd_left = (cos[2, :rows, :rows], cos[3, :rows, :rows])
    inv_right = (cos[2], cos[3])
    inv_left = (cos[0, :rows, :rows], cos[1, :rows, :rows])
    strip = lambda x: [x[:, s * wide:(s + 1) * wide] for s in range(strips)]
    coeffs = [x.astype(BF16) for x in both_sides(strip(blended), fwd_left, fwd_right, False)]

    def part(g):
        a, s = g // strips, g % strips
        return a, s

    picked = []
    for g in range(groups):
        a, s = part(g)
        own = coeffs[s][a * SPAN:(a + 1) * SPAN]
        picked.append(jnp.sum(mm(own, wide_hot[g]) * wave_hot[g], axis=0, keepdims=True))
    payload = jnp.concatenate(
        picked + [w.astype(F32) for w in wave] + [w.astype(F32) for w in wide_pos], axis=0
    ).astype(BF16)
    me = chip * nodes + node
    box[...] = payload
    recv[me] = payload

    pl.semaphore_wait(barrier, count - 1)
    peers(
        lambda off, to: pltpu.make_async_remote_copy(
            src_ref=box,
            dst_ref=recv.at[me],
            send_sem=send_sem,
            recv_sem=recv_sem.at[off],
            device_id=to,
            device_id_type=MESH,
        ).start()
    )

    sparse_rows = [[None] * strips for _ in range(rows // SPAN)]
    for g in range(groups):
        a, s = part(g)
        mask = mm_nt(wave_hot[g].astype(BF16), wide_hot[g])
        own = coeffs[s][a * SPAN:(a + 1) * SPAN].astype(F32)
        sparse_rows[a][s] = (mask * own).astype(BF16)
    sparse = [
        jnp.concatenate([row[s] for row in sparse_rows], axis=0) for s in range(strips)
    ]
    own_part = both_sides(sparse, inv_left, inv_right, True)
    for s in range(strips):
        cut = slice(s * wide, (s + 1) * wide)
        new_out[:, cut] = blended[:, cut] - own_part[s]
    store_new = pltpu.make_async_copy(new_out, new_hbm.at[0], out_sem.at[0])
    store_new.start()

    acc[...] = jnp.zeros_like(acc)
    batch = math.gcd(nodes, 8)

    def decode(start):
        block = recv[pl.ds(start, batch)].astype(F32)
        for g in range(groups):
            left, right = [], []
            for i in range(batch):
                val = block[i, g:g + 1]
                row = block[i, groups + g:groups + g + 1].astype(jnp.int32)
                col = block[i, 2 * groups + g:2 * groups + g + 1].astype(jnp.int32)
                left.append(jnp.where(tall_iota == row, val, 0.0).astype(BF16))
                right.append((wide_iota == col).astype(F32).astype(BF16))
            a, s = part(g)
            acc[pl.ds(a * SPAN, SPAN), pl.ds(s * wide, wide)] += mm_nt(
                jnp.concatenate(left, axis=1), jnp.concatenate(right, axis=1)
            )

    for off in sorted(range(chips), key=lambda o: min(o, chips - o)):
        source = lax.rem(chip + chips - off, chips) * nodes
        landed = recv.at[pl.ds(source, nodes - 1 if off == 0 else nodes)]
        pltpu.make_async_copy(landed, landed, recv_sem.at[off]).wait()
        if nodes == batch:
            decode(source)
        else:
            pl.loop(0, nodes // batch)(lambda i: decode(source + i * batch))

    totals = strip(acc[...])
    field = both_sides(totals, inv_left, inv_right, False)
    same = (
        lax.broadcasted_iota(jnp.int32, (wide, wide), 0) // SPAN
        == lax.broadcasted_iota(jnp.int32, (wide, wide), 1) // SPAN
    ).astype(F32).astype(BF16)
    for s in range(strips):
        for a in range(rows // SPAN):
            band = slice(a * SPAN, (a + 1) * SPAN)
            power = totals[s][band] * totals[s][band]
            power = jnp.sum(power.reshape(SPAN // 8, 8, wide), axis=0)
            high, low = halves(power)
            energy = jnp.sum(mm(high, same) + mm(low, same), axis=0, keepdims=True)
            scale = 1.0 / jnp.sqrt(energy * (1.0 / (SPAN * SPAN)) + 1.0)
            upd[band, s * wide:(s + 1) * wide] = field[s][band] * scale
    store_upd = pltpu.make_async_copy(upd, upd_hbm, out_sem.at[1])
    store_upd.start()

    sent = recv.at[pl.ds(0, count - 1)]
    pltpu.make_async_copy(sent, sent, send_sem).wait()
    store_new.wait()
    store_upd.wait()


def solution(mesh):
    nodes, chips = mesh.shape["node"], mesh.shape["chip"]

    def step(momentum, gradient, indices):
        _, rows, cols = momentum.shape
        spans, topk = indices.shape[1:]
        per = LANES // topk
        wide = per * SPAN
        used = 3 * (spans // per)
        cosines = jnp.asarray(cosine_blocks(per))
        hbm = pl.BlockSpec(memory_space=pl.ANY)
        return tuple(pl.pallas_call(
            functools.partial(kernel, nodes, chips, topk),
            out_shape=(
                jax.ShapeDtypeStruct((1, rows, cols), F32),
                jax.ShapeDtypeStruct((rows, cols), F32),
            ),
            in_specs=[hbm] * 4,
            out_specs=(hbm, hbm),
            scratch_shapes=[
                pltpu.VMEM((rows, cols), F32),
                pltpu.VMEM((rows, cols), BF16),
                pltpu.VMEM((spans, topk), jnp.int32),
                pltpu.VMEM((4, wide, wide), BF16),
                pltpu.VMEM((rows, cols), F32),
                pltpu.VMEM((rows, cols), F32),
                pltpu.VMEM((used, LANES), BF16),
                pltpu.VMEM((nodes * chips, used, LANES), BF16),
                pltpu.VMEM((rows, cols), F32),
                pltpu.SemaphoreType.DMA((4,)),
                pltpu.SemaphoreType.DMA((2,)),
                pltpu.SemaphoreType.DMA,
                pltpu.SemaphoreType.DMA((chips,)),
            ],
            compiler_params=pltpu.CompilerParams(collective_id=0, has_side_effects=True),
        )(momentum, gradient, indices, cosines))

    return jax.shard_map(
        step,
        mesh=mesh,
        in_specs=(P(("node", "chip"), None, None),) * 3,
        out_specs=(P(("node", "chip"), None, None), P()),
        check_vma=False,
    )
```

time: 128 us -> 18.5 us (0.14)
  waiting for transfers between devices: 39.8 us -> 0 us
  blocking collectives: 28 us -> 0 us
  local copies, waits for them, and re-layouts: 24.9 us -> 2.42 us
  matrix products: 15.8 us -> 0 us
  Pallas kernels: 0 us -> 15.2 us
  between operations: 14.2 us -> 0.65 us
  other arithmetic: 3.41 us -> 0 us
  loops' own time: 1.61 us -> 0 us
    psum x1 -> x0, waiting for transfers between devices: 39.7 us -> none  [shards(): totals = lax.psum(partial_sum, 'node')]
    all_gather x2 -> x0, blocking collectives: 28 us -> none  [the longest x1 14.8 us: shards(): lax.all_gather(indices, 'chip', axis=0, tiled=True)]
    dot_general x38 -> x0, matrix products: 15.8 us -> none  [the longest x32 8.39 us: one_span(): lax.dot_general(left_hot, right_hot, (((0,), (0,)), ((), ())), preferred_...]
    pallas_call x0 -> x1, Pallas kernels: none -> 15.2 us  [step(): pl.pallas_call(functools.partial(kernel, nodes, chips, topk), out_shape=(...]
    dynamic_update_slice x32 -> x0, local copies, waits for them, and re-layouts: 12.6 us -> none  [decode_block(): return lax.map(one_span, (values_rows, slot_rows))]
    gather x4 -> x0, local copies, waits for them, and re-layouts: 5.09 us -> none  [shards(): picked = jnp.take_along_axis(coeffs, slots, axis=1).astype(jnp.bfloat16)]
    broadcast_in_dim x64 -> x0, local copies, waits for them, and re-layouts: 3.37 us -> none  [the longest x32 2.91 us: decode_block(): return lax.map(one_span, (values_rows, slot_rows))]
    reshape x8 -> x0, local copies, waits for them, and re-layouts: 2.88 us -> none  [the longest x3 1.43 us: inverse_blocks(): blocks = coeffs.reshape(coeffs.shape[0], edge_len, edge_len)]
  transfers between devices with their start and end apart: 1 -> 0, of which waited for: 1 -> 0; matrix products, arithmetic and copies ran while one was open for 12% -> 0% of each run, Pallas kernels for 0% -> 0%
where the time goes in v1:
time: 18.5 us; the launch traced here: 18.2 us
  Pallas kernels  15.2 us (82%)
  local copies, waits for them, and re-layouts  2.42 us (13%)
  between operations  0.65 us (4%)
    pallas_call x1, Pallas kernels, step(): pl.pallas_call(functools.partial(kernel, nodes, chips, topk), out_shape=(...  15.2 us
    unnamed x4, local copies, waits for them, and re-layouts  2.42 us

profile of v1, /device:TPU:0, one launch (start us, length us, event | category | flops | bytes accessed | tf_op | source)
XLA Modules:
  0.0 18.2 jit_solution(946262568356342833)
XLA Ops:
  0.6 15.2 %shard_map.59 = (f32[1,128,512]{2,1,0:T(8,128)}, f32[128,512]{1,0:T(8,128)}) custom-call(f32[1,128,512]{2,1,0:T(8,128)} %mom_hbm.1, bf16[1,128,512]{2,1,0:T(8,128)(2,1)} %grad_hbm.1, s32[1,16,32]{2,1,0:T(8,128)} %idx_hbm.1, bf16[4,256,256]{2,1,0:T(8,128)(2,1)} %constant.2.clone.cos_hbm), custom_call_target="tpu_custom_call" | custom-call | tf_op jit(solution)/shard_map/pallas_call | solution.py:230
  15.8 0.0 copy-start
  15.8 1.7 %copy.8 = f32[1,128,512]{2,1,0:T(8,128)} copy(f32[1,128,512]{2,1,0:T(8,128)} %get-tuple-element.4) | data formatting | bytes 524288
  17.5 0.0 copy-done
  17.5 0.7 %copy.9 = f32[128,512]{1,0:T(8,128)} copy(f32[128,512]{1,0:T(8,128)S(1)} %copy-done) | data formatting | bytes 524288
Async XLA Ops:
  15.8 1.7 %copy-start = (f32[128,512]{1,0:T(8,128)S(1)}, f32[128,512]{1,0:T(8,128)}, u32[]{:S(2)}) copy-start(f32[128,512]{1,0:T(8,128)} %get-tuple-element.5) | copy-start | bytes 786436

commit v2 on v1

--- a/solution.py
+++ b/solution.py
@@ -54,8 +54,8 @@
 
 
 def kernel(
-    nodes, chips, topk, mom_hbm, grad_hbm, idx_hbm, cos_hbm, new_hbm, upd_hbm,
-    mom, grad, idx, cos, new_out, upd, box, recv, acc, in_sem, out_sem, send_sem, recv_sem,
+    nodes, chips, topk, mom_hbm, grad_hbm, idx_hbm, cos_hbm, new_out, acc, cos,
+    mom, grad, idx, box, recv, in_sem, send_sem, recv_sem,
 ):
     node, chip = lax.axis_index("node"), lax.axis_index("chip")
     count = nodes * chips
@@ -162,8 +162,6 @@
     for s in range(strips):
         cut = slice(s * wide, (s + 1) * wide)
         new_out[:, cut] = blended[:, cut] - own_part[s]
-    store_new = pltpu.make_async_copy(new_out, new_hbm.at[0], out_sem.at[0])
-    store_new.start()
 
     acc[...] = jnp.zeros_like(acc)
     batch = math.gcd(nodes, 8)
@@ -192,12 +190,27 @@
         else:
             pl.loop(0, nodes // batch)(lambda i: decode(source + i * batch))
 
-    totals = strip(acc[...])
-    field = both_sides(totals, inv_left, inv_right, False)
+    sent = recv.at[pl.ds(0, count - 1)]
+    pltpu.make_async_copy(sent, sent, send_sem).wait()
+
+
+def finish(new_in, acc, cos, new_hbm, upd_hbm, upd, sem):
+    store_new = pltpu.make_async_copy(new_in, new_hbm.at[0], sem.at[0])
+    store_new.start()
+    rows, cols = acc.shape
+    wide = cos.shape[-1]
+    strips = cols // wide
+    totals = [acc[:, s * wide:(s + 1) * wide] for s in range(strips)]
     same = (
         lax.broadcasted_iota(jnp.int32, (wide, wide), 0) // SPAN
         == lax.broadcasted_iota(jnp.int32, (wide, wide), 1) // SPAN
     ).astype(F32).astype(BF16)
+    field = both_sides(
+        totals,
+        (cos[0, :rows, :rows], cos[1, :rows, :rows]),
+        (cos[2], cos[3]),
+        False,
+    )
     for s in range(strips):
         for a in range(rows // SPAN):
             band = slice(a * SPAN, (a + 1) * SPAN)
@@ -207,11 +220,8 @@
             energy = jnp.sum(mm(high, same) + mm(low, same), axis=0, keepdims=True)
             scale = 1.0 / jnp.sqrt(energy * (1.0 / (SPAN * SPAN)) + 1.0)
             upd[band, s * wide:(s + 1) * wide] = field[s][band] * scale
-    store_upd = pltpu.make_async_copy(upd, upd_hbm, out_sem.at[1])
+    store_upd = pltpu.make_async_copy(upd, upd_hbm, sem.at[1])
     store_upd.start()
-
-    sent = recv.at[pl.ds(0, count - 1)]
-    pltpu.make_async_copy(sent, sent, send_sem).wait()
     store_new.wait()
     store_upd.wait()
 
@@ -226,32 +236,45 @@
         wide = per * SPAN
         used = 3 * (spans // per)
         cosines = jnp.asarray(cosine_blocks(per))
-        hbm = pl.BlockSpec(memory_space=pl.ANY)
+        hbm = pl.BlockSpec(memory_space=pltpu.HBM)
+        vmem = pl.BlockSpec(memory_space=pltpu.VMEM)
+        new_momentum, totals, tables = pl.pallas_call(
+            functools.partial(kernel, nodes, chips, topk),
+            out_shape=(
+                pltpu.VMEM((rows, cols), F32),
+                pltpu.VMEM((rows, cols), F32),
+                pltpu.VMEM((4, wide, wide), BF16),
+            ),
+            in_specs=[hbm] * 4,
+            out_specs=(vmem, vmem, vmem),
+            scratch_shapes=[
+                pltpu.VMEM((rows, cols), F32),
+                pltpu.VMEM((rows, cols), BF16),
+                pltpu.VMEM((spans, topk), jnp.int32),
+                pltpu.VMEM((used, LANES), BF16),
+                pltpu.VMEM((nodes * chips, used, LANES), BF16),
+                pltpu.SemaphoreType.DMA((4,)),
+                pltpu.SemaphoreType.DMA,
+                pltpu.SemaphoreType.DMA((chips,)),
+            ],
+            compiler_params=pltpu.CompilerParams(
+                collective_id=0, has_side_effects=True, vmem_limit_bytes=24 * 2**20
+            ),
+        )(*(pltpu.with_memory_space_constraint(x, pltpu.HBM) for x in (momentum, gradient, indices, cosines)))
         return tuple(pl.pallas_call(
-            functools.partial(kernel, nodes, chips, topk),
+            finish,
             out_shape=(
                 jax.ShapeDtypeStruct((1, rows, cols), F32),
                 jax.ShapeDtypeStruct((rows, cols), F32),
             ),
-            in_specs=[hbm] * 4,
+            in_specs=[vmem, vmem, vmem],
             out_specs=(hbm, hbm),
             scratch_shapes=[
                 pltpu.VMEM((rows, cols), F32),
-                pltpu.VMEM((rows, cols), BF16),
-                pltpu.VMEM((spans, topk), jnp.int32),
-                pltpu.VMEM((4, wide, wide), BF16),
-                pltpu.VMEM((rows, cols), F32),
-                pltpu.VMEM((rows, cols), F32),
-                pltpu.VMEM((used, LANES), BF16),
-                pltpu.VMEM((nodes * chips, used, LANES), BF16),
-                pltpu.VMEM((rows, cols), F32),
-                pltpu.SemaphoreType.DMA((4,)),
                 pltpu.SemaphoreType.DMA((2,)),
-                pltpu.SemaphoreType.DMA,
-                pltpu.SemaphoreType.DMA((chips,)),
             ],
-            compiler_params=pltpu.CompilerParams(collective_id=0, has_side_effects=True),
-        )(momentum, gradient, indices, cosines))
+            compiler_params=pltpu.CompilerParams(vmem_limit_bytes=24 * 2**20),
+        )(new_momentum, totals, tables))
 
     return jax.shard_map(
         step,

time: 18.5 us -> 16.3 us (0.88)
  local copies, waits for them, and re-layouts: 2.42 us -> 0 us
  Pallas kernels: 15.2 us -> 15.4 us
    unnamed x4 -> x0, local copies, waits for them, and re-layouts: 2.42 us -> none
    pallas_call x0 -> x1, Pallas kernels: none -> 1.64 us  [step(): pl.pallas_call(finish, out_shape=(jax.ShapeDtypeStruct((1, rows, cols), F...]
    pallas_call x1, Pallas kernels: 15.2 us -> 13.8 us  [step(): pl.pallas_call(functools.partial(kernel, nodes, chips, topk), out_shape=(...]
where the time goes in v2:
time: 16.3 us; the launch traced here: 16.1 us
  Pallas kernels  15.4 us (94%)
  between operations  0.64 us (4%)
    pallas_call x1, Pallas kernels, step(): pl.pallas_call(functools.partial(kernel, nodes, chips, topk), out_shape=(...  13.8 us
    pallas_call x1, Pallas kernels, step(): pl.pallas_call(finish, out_shape=(jax.ShapeDtypeStruct((1, rows, cols), F...  1.64 us

profile of v2, /device:TPU:0, one launch (start us, length us, event | category | flops | bytes accessed | tf_op | source)
XLA Modules:
  0.0 16.1 jit_solution(9413226485469104819)
XLA Ops:
  0.6 13.8 %shard_map.59 = (f32[128,512]{1,0:T(8,128)S(1)}, f32[128,512]{1,0:T(8,128)S(1)}, bf16[4,256,256]{2,1,0:T(8,128)(2,1)S(1)}) custom-call(f32[1,128,512]{2,1,0:T(8,128)} %mom_hbm.1, bf16[1,128,512]{2,1,0:T(8,128)(2,1)} %grad_hbm.1, s32[1,16,32]{2,1,0:T(8,128)} %idx_hbm.1, bf16[4,256,256]{2,1,0:T(8,128)(2,1)} %constant.2.clone.cos_hbm), custom_call_target="tpu_custom_call" | custom-call | tf_op jit(solution)/shard_map/pallas_call | solution.py:241
  14.4 1.6 %shard_map.60 = (f32[1,128,512]{2,1,0:T(8,128)}, f32[128,512]{1,0:T(8,128)}) custom-call(f32[128,512]{1,0:T(8,128)S(1)} %get-tuple-element.5.new_in, f32[128,512]{1,0:T(8,128)S(1)} %get-tuple-element.6.acc, bf16[4,256,256]{2,1,0:T(8,128)(2,1)S(1)} %get-tuple-element.7.cos), custom_call_target="tpu_custom_call" | custom-call | tf_op jit(solution)/shard_map/pallas_call | solution.py:264

commit v3 on v2

--- a/solution.py
+++ b/solution.py
@@ -40,14 +40,11 @@
     return lax.dot_general(a, b, (((1,), (1,)), ((), ())), preferred_element_type=F32)
 
 
-def both_sides(blocks, left, right, exact):
+def both_sides(blocks, left, right):
     outs = []
     for x in blocks:
-        if exact:
-            y = mm(x, right[0]) + mm(x, right[1])
-        else:
-            high, low = halves(x)
-            y = mm(high, right[0]) + (mm(low, right[0]) + mm(high, right[1]))
+        high, low = halves(x)
+        y = mm(high, right[0]) + (mm(low, right[0]) + mm(high, right[1]))
         high, low = halves(y)
         outs.append(mm(left[0], high) + (mm(left[0], low) + mm(left[1], high)))
     return outs
@@ -69,7 +66,13 @@
     loads = [
         pltpu.make_async_copy(src, dst, in_sem.at[i])
         for i, (src, dst) in enumerate(
-            ((idx_hbm.at[0], idx), (mom_hbm.at[0], mom), (grad_hbm.at[0], grad), (cos_hbm, cos))
+            (
+                (idx_hbm.at[0], idx),
+                (cos_hbm.at[pl.ds(0, 2)], cos.at[pl.ds(0, 2)]),
+                (mom_hbm.at[0], mom),
+                (grad_hbm.at[0], grad),
+                (cos_hbm.at[pl.ds(2, 2)], cos.at[pl.ds(2, 2)]),
+            )
         )
     ]
     for load in loads:
@@ -77,22 +80,27 @@
 
     barrier = pltpu.get_barrier_semaphore()
 
+    high_side = 2 * chip >= chips
+
+    def plane(t):
+        up = t + (chip <= t).astype(jnp.int32)
+        down = chips - 1 - t
+        return jnp.where(high_side, up, down - (down <= chip).astype(jnp.int32))
+
     def peers(visit):
-        def one(off, i):
-            to_node = lax.rem(node + i, nodes)
-            to_chip = lax.rem(chip + off, chips)
-            visit(off, {"node": to_node, "chip": to_chip})
-
-        order = sorted(range(chips), key=lambda o: -min(o, chips - o))
-        for off in order:
-            first = 1 if off == 0 else 0
+        def one(to_chip, base, i):
+            visit({"node": lax.rem(base + i, nodes), "chip": to_chip})
+
+        for t in range(chips):
+            own = t == chips - 1
+            go = functools.partial(one, *((chip, node) if own else (plane(t), nodes - 1 - node)))
             if nodes <= 8:
-                for i in range(first, nodes):
-                    one(off, i)
+                for i in range(1 if own else 0, nodes):
+                    go(i)
             else:
-                pl.loop(first, nodes)(functools.partial(one, off))
-
-    peers(lambda off, to: pl.semaphore_signal(barrier, inc=1, device_id=to, device_id_type=MESH))
+                pl.loop(1 if own else 0, nodes)(go)
+
+    peers(lambda to: pl.semaphore_signal(barrier, inc=1, device_id=to, device_id_type=MESH))
 
     loads[0].wait()
     slots = idx[...]
@@ -108,28 +116,33 @@
     wide_pos = [(x // (SPAN * SPAN)) * SPAN + x % SPAN for x in lists]
     tall_iota = lax.broadcasted_iota(jnp.int32, (SPAN, LANES), 0)
     wide_iota = lax.broadcasted_iota(jnp.int32, (wide, LANES), 0)
-    wave_hot = [(tall_iota == w).astype(F32) for w in wave]
+    wave_hot = [(tall_iota == w).astype(F32).astype(BF16) for w in wave]
     wide_hot = [(wide_iota == w).astype(F32).astype(BF16) for w in wide_pos]
 
-    for load in loads[1:]:
-        load.wait()
+    loads[1].wait()
+    tall_cos = [
+        mm(cos[0, :SPAN, :SPAN], hot) + mm(cos[1, :SPAN, :SPAN], hot) for hot in wave_hot
+    ]
+    wide_high = [mm(cos[0], hot).astype(BF16) for hot in wide_hot]
+    wide_low = [mm(cos[1], hot).astype(BF16) for hot in wide_hot]
+
+    loads[2].wait()
+    loads[3].wait()
     blended = 0.9 * mom[...] + grad[...].astype(F32)
-    fwd_right = (cos[0], cos[1])
-    fwd_left = (cos[2, :rows, :rows], cos[3, :rows, :rows])
-    inv_right = (cos[2], cos[3])
-    inv_left = (cos[0, :rows, :rows], cos[1, :rows, :rows])
-    strip = lambda x: [x[:, s * wide:(s + 1) * wide] for s in range(strips)]
-    coeffs = [x.astype(BF16) for x in both_sides(strip(blended), fwd_left, fwd_right, False)]
 
     def part(g):
         a, s = g // strips, g % strips
         return a, s
 
+    def region(g):
+        a, s = part(g)
+        return slice(a * SPAN, (a + 1) * SPAN), slice(s * wide, (s + 1) * wide)
+
     picked = []
     for g in range(groups):
-        a, s = part(g)
-        own = coeffs[s][a * SPAN:(a + 1) * SPAN]
-        picked.append(jnp.sum(mm(own, wide_hot[g]) * wave_hot[g], axis=0, keepdims=True))
+        high, low = halves(blended[region(g)])
+        sums = mm(high, wide_high[g]) + (mm(low, wide_high[g]) + mm(high, wide_low[g]))
+        picked.append(jnp.sum(sums * tall_cos[g], axis=0, keepdims=True))
     payload = jnp.concatenate(
         picked + [w.astype(F32) for w in wave] + [w.astype(F32) for w in wide_pos], axis=0
     ).astype(BF16)
@@ -139,29 +152,23 @@
 
     pl.semaphore_wait(barrier, count - 1)
     peers(
-        lambda off, to: pltpu.make_async_remote_copy(
+        lambda to: pltpu.make_async_remote_copy(
             src_ref=box,
             dst_ref=recv.at[me],
             send_sem=send_sem,
-            recv_sem=recv_sem.at[off],
+            recv_sem=recv_sem.at[chip],
             device_id=to,
             device_id_type=MESH,
         ).start()
     )
 
-    sparse_rows = [[None] * strips for _ in range(rows // SPAN)]
     for g in range(groups):
-        a, s = part(g)
-        mask = mm_nt(wave_hot[g].astype(BF16), wide_hot[g])
-        own = coeffs[s][a * SPAN:(a + 1) * SPAN].astype(F32)
-        sparse_rows[a][s] = (mask * own).astype(BF16)
-    sparse = [
-        jnp.concatenate([row[s] for row in sparse_rows], axis=0) for s in range(strips)
-    ]
-    own_part = both_sides(sparse, inv_left, inv_right, True)
-    for s in range(strips):
-        cut = slice(s * wide, (s + 1) * wide)
-        new_out[:, cut] = blended[:, cut] - own_part[s]
+        sent_value = picked[g].astype(BF16).astype(F32)
+        high, low = halves(tall_cos[g] * sent_value)
+        own_part = mm_nt(high, wide_high[g]) + (
+            mm_nt(low, wide_high[g]) + mm_nt(high, wide_low[g])
+        )
+        new_out[region(g)] = blended[region(g)] - own_part
 
     acc[...] = jnp.zeros_like(acc)
     batch = math.gcd(nodes, 8)
@@ -181,15 +188,17 @@
                 jnp.concatenate(left, axis=1), jnp.concatenate(right, axis=1)
             )
 
-    for off in sorted(range(chips), key=lambda o: min(o, chips - o)):
-        source = lax.rem(chip + chips - off, chips) * nodes
-        landed = recv.at[pl.ds(source, nodes - 1 if off == 0 else nodes)]
-        pltpu.make_async_copy(landed, landed, recv_sem.at[off]).wait()
+    for t in reversed(range(chips)):
+        source = chip if t == chips - 1 else plane(t)
+        first = source * nodes
+        landed = recv.at[pl.ds(first, nodes - 1 if t == chips - 1 else nodes)]
+        pltpu.make_async_copy(landed, landed, recv_sem.at[source]).wait()
         if nodes == batch:
-            decode(source)
+            decode(first)
         else:
-            pl.loop(0, nodes // batch)(lambda i: decode(source + i * batch))
-
+            pl.loop(0, nodes // batch)(lambda i: decode(first + i * batch))
+
+    loads[4].wait()
     sent = recv.at[pl.ds(0, count - 1)]
     pltpu.make_async_copy(sent, sent, send_sem).wait()
 
@@ -209,7 +218,6 @@
         totals,
         (cos[0, :rows, :rows], cos[1, :rows, :rows]),
         (cos[2], cos[3]),
-        False,
     )
     for s in range(strips):
         for a in range(rows // SPAN):
@@ -253,7 +261,7 @@
                 pltpu.VMEM((spans, topk), jnp.int32),
                 pltpu.VMEM((used, LANES), BF16),
                 pltpu.VMEM((nodes * chips, used, LANES), BF16),
-                pltpu.SemaphoreType.DMA((4,)),
+                pltpu.SemaphoreType.DMA((5,)),
                 pltpu.SemaphoreType.DMA,
                 pltpu.SemaphoreType.DMA((chips,)),
             ],

time: 16.3 us -> 15.2 us (0.933)
  Pallas kernels: 15.4 us -> 14.4 us
    pallas_call x1, Pallas kernels: 13.8 us -> 12.7 us  [step(): pl.pallas_call(functools.partial(kernel, nodes, chips, topk), out_shape=(...]
where the time goes in v3:
time: 15.2 us; the launch traced here: 15 us
  Pallas kernels  14.4 us (95%)
  between operations  0.64 us (4%)
    pallas_call x1, Pallas kernels, step(): pl.pallas_call(functools.partial(kernel, nodes, chips, topk), out_shape=(...  12.7 us
    pallas_call x1, Pallas kernels, step(): pl.pallas_call(finish, out_shape=(jax.ShapeDtypeStruct((1, rows, cols), F...  1.64 us

profile of v3, /device:TPU:0, one launch (start us, length us, event | category | flops | bytes accessed | tf_op | source)
XLA Modules:
  0.0 15.0 jit_solution(10800836473518155347)
XLA Ops:
  0.6 12.7 %shard_map.59 = (f32[128,512]{1,0:T(8,128)S(1)}, f32[128,512]{1,0:T(8,128)S(1)}, bf16[4,256,256]{2,1,0:T(8,128)(2,1)S(1)}) custom-call(f32[1,128,512]{2,1,0:T(8,128)} %mom_hbm.1, bf16[1,128,512]{2,1,0:T(8,128)(2,1)} %grad_hbm.1, s32[1,16,32]{2,1,0:T(8,128)} %idx_hbm.1, bf16[4,256,256]{2,1,0:T(8,128)(2,1)} %constant.2.clone.cos_hbm), custom_call_target="tpu_custom_call" | custom-call | tf_op jit(solution)/shard_map/pallas_call | solution.py:249
  13.4 1.6 %shard_map.60 = (f32[1,128,512]{2,1,0:T(8,128)}, f32[128,512]{1,0:T(8,128)}) custom-call(f32[128,512]{1,0:T(8,128)S(1)} %get-tuple-element.5.new_in, f32[128,512]{1,0:T(8,128)S(1)} %get-tuple-element.6.acc, bf16[4,256,256]{2,1,0:T(8,128)(2,1)S(1)} %get-tuple-element.7.cos), custom_call_target="tpu_custom_call" | custom-call | tf_op jit(solution)/shard_map/pallas_call | solution.py:272

commit v4 on v3

--- a/solution.py
+++ b/solution.py
@@ -81,6 +81,7 @@
     barrier = pltpu.get_barrier_semaphore()
 
     high_side = 2 * chip >= chips
+    half = nodes // 2 if nodes % 2 == 0 else nodes
 
     def plane(t):
         up = t + (chip <= t).astype(jnp.int32)
@@ -89,7 +90,8 @@
 
     def peers(visit):
         def one(to_chip, base, i):
-            visit({"node": lax.rem(base + i, nodes), "chip": to_chip})
+            spot = base + i
+            visit({"node": jnp.where(spot >= nodes, spot - nodes, spot), "chip": to_chip})
 
         for t in range(chips):
             own = t == chips - 1
@@ -156,7 +158,7 @@
             src_ref=box,
             dst_ref=recv.at[me],
             send_sem=send_sem,
-            recv_sem=recv_sem.at[chip],
+            recv_sem=recv_sem.at[chip, node // half],
             device_id=to,
             device_id_type=MESH,
         ).start()
@@ -171,7 +173,7 @@
         new_out[region(g)] = blended[region(g)] - own_part
 
     acc[...] = jnp.zeros_like(acc)
-    batch = math.gcd(nodes, 8)
+    batch = math.gcd(half, 8)
 
     def decode(start):
         block = recv[pl.ds(start, batch)].astype(F32)
@@ -190,13 +192,17 @@
 
     for t in reversed(range(chips)):
         source = chip if t == chips - 1 else plane(t)
-        first = source * nodes
-        landed = recv.at[pl.ds(first, nodes - 1 if t == chips - 1 else nodes)]
-        pltpu.make_async_copy(landed, landed, recv_sem.at[source]).wait()
-        if nodes == batch:
-            decode(first)
-        else:
-            pl.loop(0, nodes // batch)(lambda i: decode(first + i * batch))
+        for h in range(nodes // half):
+            part_no = lax.rem(node // half + h, nodes // half)
+            first = source * nodes + part_no * half
+            own = t == chips - 1 and h == 0
+            if not (own and half == 1):
+                landed = recv.at[pl.ds(first, half - 1 if own else half)]
+                pltpu.make_async_copy(landed, landed, recv_sem.at[source, part_no]).wait()
+            if half == batch:
+                decode(first)
+            else:
+                pl.loop(0, half // batch)(lambda i: decode(first + i * batch))
 
     loads[4].wait()
     sent = recv.at[pl.ds(0, count - 1)]
@@ -214,24 +220,26 @@
         lax.broadcasted_iota(jnp.int32, (wide, wide), 0) // SPAN
         == lax.broadcasted_iota(jnp.int32, (wide, wide), 1) // SPAN
     ).astype(F32).astype(BF16)
-    field = both_sides(
-        totals,
-        (cos[0, :rows, :rows], cos[1, :rows, :rows]),
-        (cos[2], cos[3]),
-    )
+    left = (cos[0, :rows, :rows], cos[1, :rows, :rows])
+    stores = [store_new]
     for s in range(strips):
+        scales = []
         for a in range(rows // SPAN):
-            band = slice(a * SPAN, (a + 1) * SPAN)
-            power = totals[s][band] * totals[s][band]
-            power = jnp.sum(power.reshape(SPAN // 8, 8, wide), axis=0)
+            power = totals[s][a * SPAN:(a + 1) * SPAN]
+            power = jnp.sum((power * power).reshape(SPAN // 8, 8, wide), axis=0)
             high, low = halves(power)
             energy = jnp.sum(mm(high, same) + mm(low, same), axis=0, keepdims=True)
-            scale = 1.0 / jnp.sqrt(energy * (1.0 / (SPAN * SPAN)) + 1.0)
-            upd[band, s * wide:(s + 1) * wide] = field[s][band] * scale
-    store_upd = pltpu.make_async_copy(upd, upd_hbm, sem.at[1])
-    store_upd.start()
-    store_new.wait()
-    store_upd.wait()
+            scales.append(1.0 / jnp.sqrt(energy * (1.0 / (SPAN * SPAN)) + 1.0))
+        field = both_sides([totals[s]], left, (cos[2], cos[3]))[0]
+        cut = pl.ds(s * wide, wide)
+        for a, scale in enumerate(scales):
+            band = slice(a * SPAN, (a + 1) * SPAN)
+            upd[band, s * wide:(s + 1) * wide] = field[band] * scale
+        store = pltpu.make_async_copy(upd.at[:, cut], upd_hbm.at[:, cut], sem.at[1 + s])
+        store.start()
+        stores.append(store)
+    for store in stores:
+        store.wait()
 
 
 def solution(mesh):
@@ -263,7 +271,7 @@
                 pltpu.VMEM((nodes * chips, used, LANES), BF16),
                 pltpu.SemaphoreType.DMA((5,)),
                 pltpu.SemaphoreType.DMA,
-                pltpu.SemaphoreType.DMA((chips,)),
+                pltpu.SemaphoreType.DMA((chips, 2)),
             ],
             compiler_params=pltpu.CompilerParams(
                 collective_id=0, has_side_effects=True, vmem_limit_bytes=24 * 2**20
@@ -279,7 +287,7 @@
             out_specs=(hbm, hbm),
             scratch_shapes=[
                 pltpu.VMEM((rows, cols), F32),
-                pltpu.SemaphoreType.DMA((2,)),
+                pltpu.SemaphoreType.DMA((1 + cols // wide,)),
             ],
             compiler_params=pltpu.CompilerParams(vmem_limit_bytes=24 * 2**20),
         )(new_momentum, totals, tables))

time: 15.2 us -> 15.1 us (level)
  Pallas kernels: 14.4 us -> 14.2 us
where the time goes in v4:
time: 15.1 us; the launch traced here: 14.8 us
  Pallas kernels  14.2 us (94%)
  between operations  0.64 us (4%)
    pallas_call x1, Pallas kernels, step(): pl.pallas_call(functools.partial(kernel, nodes, chips, topk), out_shape=(...  12.6 us
    pallas_call x1, Pallas kernels, step(): pl.pallas_call(finish, out_shape=(jax.ShapeDtypeStruct((1, rows, cols), F...  1.61 us

profile of v4, /device:TPU:0, one launch (start us, length us, event | category | flops | bytes accessed | tf_op | source)
XLA Modules:
  0.0 14.8 jit_solution(9752256657339314348)
XLA Ops:
  0.6 12.6 %shard_map.59 = (f32[128,512]{1,0:T(8,128)S(1)}, f32[128,512]{1,0:T(8,128)S(1)}, bf16[4,256,256]{2,1,0:T(8,128)(2,1)S(1)}) custom-call(f32[1,128,512]{2,1,0:T(8,128)} %mom_hbm.1, bf16[1,128,512]{2,1,0:T(8,128)(2,1)} %grad_hbm.1, s32[1,16,32]{2,1,0:T(8,128)} %idx_hbm.1, bf16[4,256,256]{2,1,0:T(8,128)(2,1)} %constant.2.clone.cos_hbm), custom_call_target="tpu_custom_call" | custom-call | tf_op jit(solution)/shard_map/pallas_call | solution.py:257
  13.2 1.6 %shard_map.60 = (f32[1,128,512]{2,1,0:T(8,128)}, f32[128,512]{1,0:T(8,128)}) custom-call(f32[128,512]{1,0:T(8,128)S(1)} %get-tuple-element.5.new_in, f32[128,512]{1,0:T(8,128)S(1)} %get-tuple-element.6.acc, bf16[4,256,256]{2,1,0:T(8,128)(2,1)S(1)} %get-tuple-element.7.cos), custom_call_target="tpu_custom_call" | custom-call | tf_op jit(solution)/shard_map/pallas_call | solution.py:280

commit v5 on v4

--- a/solution.py
+++ b/solution.py
@@ -125,8 +125,14 @@
     tall_cos = [
         mm(cos[0, :SPAN, :SPAN], hot) + mm(cos[1, :SPAN, :SPAN], hot) for hot in wave_hot
     ]
-    wide_high = [mm(cos[0], hot).astype(BF16) for hot in wide_hot]
-    wide_low = [mm(cos[1], hot).astype(BF16) for hot in wide_hot]
+    edge = cos.shape[-1]
+
+    def columns(table, hot):
+        pieces = [mm(table, hot[p:p + edge]).astype(BF16) for p in range(0, wide, edge)]
+        return jnp.concatenate(pieces, axis=0)
+
+    wide_high = [columns(cos[0], hot) for hot in wide_hot]
+    wide_low = [columns(cos[1], hot) for hot in wide_hot]
 
     loads[2].wait()
     loads[3].wait()
@@ -251,7 +257,7 @@
         per = LANES // topk
         wide = per * SPAN
         used = 3 * (spans // per)
-        cosines = jnp.asarray(cosine_blocks(per))
+        cosines = jnp.asarray(cosine_blocks(2))
         hbm = pl.BlockSpec(memory_space=pltpu.HBM)
         vmem = pl.BlockSpec(memory_space=pltpu.VMEM)
         new_momentum, totals, tables = pl.pallas_call(
@@ -259,7 +265,7 @@
             out_shape=(
                 pltpu.VMEM((rows, cols), F32),
                 pltpu.VMEM((rows, cols), F32),
-                pltpu.VMEM((4, wide, wide), BF16),
+                pltpu.VMEM((4, 2 * SPAN, 2 * SPAN), BF16),
             ),
             in_specs=[hbm] * 4,
             out_specs=(vmem, vmem, vmem),
@@ -287,7 +293,7 @@
             out_specs=(hbm, hbm),
             scratch_shapes=[
                 pltpu.VMEM((rows, cols), F32),
-                pltpu.SemaphoreType.DMA((1 + cols // wide,)),
+                pltpu.SemaphoreType.DMA((1 + cols // (2 * SPAN),)),
             ],
             compiler_params=pltpu.CompilerParams(vmem_limit_bytes=24 * 2**20),
         )(new_momentum, totals, tables))

time: 15.1 us -> 14.8 us (0.980)
  Pallas kernels: 14.2 us -> 13.9 us
    pallas_call x1, Pallas kernels: 1.61 us -> 1.36 us  [step(): pl.pallas_call(finish, out_shape=(jax.ShapeDtypeStruct((1, rows, cols), F...]
where the time goes in v5:
time: 14.8 us; the launch traced here: 14.6 us
  Pallas kernels  13.9 us (94%)
  between operations  0.64 us (4%)
    pallas_call x1, Pallas kernels, step(): pl.pallas_call(functools.partial(kernel, nodes, chips, topk), out_shape=(...  12.6 us
    pallas_call x1, Pallas kernels, step(): pl.pallas_call(finish, out_shape=(jax.ShapeDtypeStruct((1, rows, cols), F...  1.36 us

profile of v5, /device:TPU:0, one launch (start us, length us, event | category | flops | bytes accessed | tf_op | source)
XLA Modules:
  0.0 14.6 jit_solution(17316388678672441427)
XLA Ops:
  0.6 12.6 %shard_map.59 = (f32[128,512]{1,0:T(8,128)S(1)}, f32[128,512]{1,0:T(8,128)S(1)}, bf16[4,128,128]{2,1,0:T(8,128)(2,1)S(1)}) custom-call(f32[1,128,512]{2,1,0:T(8,128)} %mom_hbm.1, bf16[1,128,512]{2,1,0:T(8,128)(2,1)} %grad_hbm.1, s32[1,16,32]{2,1,0:T(8,128)} %idx_hbm.1, bf16[4,128,128]{2,1,0:T(8,128)(2,1)} %constant.2.clone.cos_hbm), custom_call_target="tpu_custom_call" | custom-call | tf_op jit(solution)/shard_map/pallas_call | solution.py:263
  13.2 1.4 %shard_map.60 = (f32[1,128,512]{2,1,0:T(8,128)}, f32[128,512]{1,0:T(8,128)}) custom-call(f32[128,512]{1,0:T(8,128)S(1)} %get-tuple-element.5.new_in, f32[128,512]{1,0:T(8,128)S(1)} %get-tuple-element.6.acc, bf16[4,128,128]{2,1,0:T(8,128)(2,1)S(1)} %get-tuple-element.7.cos), custom_call_target="tpu_custom_call" | custom-call | tf_op jit(solution)/shard_map/pallas_call | solution.py:286
